TPU v7x, 512 devices: a whole 4x8x8 slice. The times are simulated.
512 devices in a mesh: agent: 16 (over x, z_lo, core), tp: 32 (over z_hi, y).
Axes of the slice: x: 4, y: 8, z: 8 (z_hi: 4, z_lo: 2; z = z_hi * 2 + z_lo), core: 2. Of those that a mesh axis runs over, the one named last changes fastest.
Arguments:
- tokens: bfloat16 [16, 512, 2048], P('agent', 'tp'), may hold values from -6 to 6
- targets: bfloat16 [16, 512, 2048], P('agent', 'tp'), may hold values from -6 to 6
- params: bfloat16 [16, 2048, 8192], P('agent', None, 'tp'), may hold values from -6 to 6
- tracker: bfloat16 [16, 2048, 8192], P('agent', None, 'tp'), may hold values from -6 to 6
- up_weight: bfloat16 [2048, 8192], P('agent', 'tp'), may hold values from -0.125 to 0.125
- down_weight: bfloat16 [8192, 2048], P('tp', 'agent'), may hold values from -0.0625 to 0.0625
- edge_weight: float32 [16], replicated, may hold values from 0.1 to 0.4
- step_size: float32 [1], replicated, may hold values from 0.1 to 0.5
Outputs:
- new_params: bfloat16 [16, 2048, 8192], P('agent', None, 'tp')
- new_tracker: bfloat16 [16, 2048, 8192], P('agent', None, 'tp')
All inputs are finite; a program needn't handle non-finite values.
Results may differ from a plain program's by a relative error of at most 0.033.
Values may be sent and summed in bfloat16 or wider, within the bound.
A program may use at most 64 MiB of HBM per device.

v0:
```python
import jax
import jax.numpy as jnp
from jax import lax
from jax.sharding import Mesh
from jax.sharding import PartitionSpec as P

TP = ("tp_0", "tp_1")


def passed_along(value, axis, steps):
    count = lax.axis_size(axis)
    pairs = [(source, (source + steps) % count) for source in range(count)]
    return lax.ppermute(value, axis, pairs)


def gather_turned(arrays, axis, dims):
    turned = [jnp.moveaxis(a, dim, 0) for a, dim in zip(arrays, dims)]
    widths = [t[0].size for t in turned]
    both = jnp.concatenate([t.reshape(-1, w) for t, w in zip(turned, widths)], axis=1)
    out = lax.all_gather(both, axis, axis=0, tiled=True)
    pieces = jnp.split(out, [sum(widths[:k]) for k in range(1, len(widths))], axis=1)
    return tuple(
        (
            jnp.moveaxis(b.reshape(-1, *t.shape[1:]), 0, dim)
            for b, t, dim in zip(pieces, turned, dims)
        )
    )


def side_by_side(arrays, axis, dim, along):
    widths = [a.shape[along] for a in arrays]
    both = jnp.concatenate(arrays, axis=along)
    out = lax.all_gather(both, axis, axis=dim, tiled=True)
    return tuple(jnp.split(out, [sum(widths[:k]) for k in range(1, len(widths))], axis=along))


def sum_in_order(pieces, axes, turns):
    lengths = [lax.axis_size(a) for a in axes]
    pieces = pieces.reshape(*lengths, *pieces.shape[1:])
    pieces = pieces.transpose(*turns, *range(len(axes), pieces.ndim))
    pieces = pieces.reshape(-1, *pieces.shape[len(axes) :])
    for k in turns:
        pieces = lax.psum_scatter(pieces, axes[k], scatter_dimension=0, tiled=True)
    return pieces[0]


def cut_along(array, dim, devices):
    before, after = (array.shape[:dim], array.shape[dim + 1 :])
    return jnp.moveaxis(array.reshape(*before, devices, -1, *after), dim, 0)


def sum_by_axis(array, axes, turns, dim):
    devices = lax.axis_size(axes)
    return sum_in_order(cut_along(array, dim, devices), axes, turns)


def joined_along(pieces, dim):
    lengths = list(pieces.shape[1:])
    lengths[dim] *= pieces.shape[0]
    return jnp.moveaxis(pieces, 0, dim).reshape(lengths)


def gather_in_order(array, axes, turns):
    pieces = array[None]
    for k in turns:
        pieces = lax.all_gather(pieces, axes[k], axis=0, tiled=True)
    block = [lax.axis_size(axes[k]) for k in reversed(turns)]
    pieces = pieces.reshape(*block, *array.shape)
    turned = sorted(range(len(turns)), key=lambda place: turns[len(turns) - 1 - place])
    return pieces.transpose(*turned, *range(len(turns), pieces.ndim)).reshape(-1, *array.shape)


def gather_axes(array, axes, turns, dim):
    return joined_along(gather_in_order(array, axes, turns), dim)


def on_device(tokens, targets, params, tracker, up_weight, down_weight, edge_weight, step_size):
    target_rows = targets[0]
    param = params[0]
    track = tracker[0]
    left_x, left_y = passed_along((param, track), "agent", 1)
    right_x, right_y = passed_along((param, track), "agent", -1)
    up_full, down_full = gather_turned((up_weight, down_weight), "agent", (0, 1))
    whole, whole_targets = side_by_side((tokens[0], target_rows), TP, 0, 1)
    scale = 1.0 / whole.shape[1] ** 0.5
    up = jnp.dot(whole, up_full, preferred_element_type=jnp.float32)

    def dgate_of(weights):
        gate = jnp.dot(whole, weights, preferred_element_type=jnp.float32) * scale
        sig = jax.nn.sigmoid(gate)
        hidden = (sig * gate * up).astype(jnp.bfloat16)
        partial_value = jnp.dot(hidden, down_full, preferred_element_type=jnp.float32)
        summed = sum_by_axis(partial_value.astype(jnp.bfloat16), TP, (1, 0), 0).astype(jnp.float32)
        local_err = (2.0 * (summed - target_rows.astype(jnp.float32))).astype(jnp.bfloat16)
        err = gather_axes(local_err, TP, (0, 1), 0)
        back = lax.dot_general(
            err, down_full, (((1,), (1,)), ((), ())), preferred_element_type=jnp.float32
        )
        return (back * up * sig * (1.0 + gate * (1.0 - sig))).astype(jnp.bfloat16)

    def weight_grad(dgate):
        return lax.dot_general(
            whole, dgate, (((0,), (0,)), ((), ())), preferred_element_type=jnp.float32
        )

    old_grad = weight_grad(dgate_of(param))
    count = lax.axis_size("agent")
    index = lax.axis_index("agent")
    e_right = lax.dynamic_slice_in_dim(edge_weight, index, 1)[0]
    e_left = lax.dynamic_slice_in_dim(edge_weight, (index + count - 1) % count, 1)[0]
    own = 1.0 - e_right - e_left
    track32 = track.astype(jnp.float32)
    mixed_x = (
        own * param.astype(jnp.float32)
        + e_right * right_x.astype(jnp.float32)
        + e_left * left_x.astype(jnp.float32)
    )
    mixed_y = (
        own * track32 + e_right * right_y.astype(jnp.float32) + e_left * left_y.astype(jnp.float32)
    )
    fresh = (mixed_x - step_size[0] * track32).astype(jnp.bfloat16)
    new_grad = weight_grad(dgate_of(fresh))
    fresh_track = (mixed_y + (new_grad - old_grad) * scale).astype(jnp.bfloat16)
    return (fresh[None], fresh_track[None])


def solution(mesh):
    finer = Mesh(mesh.devices.reshape(mesh.shape["agent"], 4, 8), ("agent", "tp_0", "tp_1"))
    in_specs = (
        P("agent", TP, None),
        P("agent", TP, None),
        P("agent", None, TP),
        P("agent", None, TP),
        P("agent", TP),
        P(TP, "agent"),
        P(),
        P(),
    )
    out_specs = (P("agent", None, TP), P("agent", None, TP))
    return jax.shard_map(
        on_device, mesh=finer, in_specs=in_specs, out_specs=out_specs, check_vma=False
    )
```

profile of v0, /device:TPU:2, one launch (start us, length us, event | category | flops | bytes accessed | tf_op | source)
XLA Modules:
  0.0 443.6 jit_solution(4100841673525199849)
XLA Ops:
  11.4 3.7 collective-permute-start
  15.1 1.9 collective-permute-start.1
  20.2 18.2 %collective-permute-done = bf16[2048,256]{1,0:T(8,128)(2,1)S(1)} collective-permute-done((bf16[2048,256]{1,0:T(8,128)(2,1)}, bf16[2048,256]{1,0:T(8,128)(2,1)S(1)}, u32[]{:S(2)}, u32[]{:S(2)}) %collective-permute-start) | collective-permute-done | bytes 1048608 | tf_op jit(solution)/shard_map/ppermute | solution.py:13
  38.4 4.3 collective-permute-done.1
  42.6 3.5 fusion.2
  46.1 73.3 %all-gather.5.cloned.1.call-done = bf16[512,4096]{1,0:T(8,128)(2,1)} async-done(((bf16[16,4096]{1,0:T(8,128)(2,1)}), bf16[512,4096]{1,0:T(8,128)(2,1)}) %all-gather.5.cloned.1.call-update) | async-done | bytes 4194320 | tf_op jit(solution)/shard_map/all_gather | solution.py:33
  119.5 2.3 convolution_multiply_fusion.3
  121.8 37.5 %all-gather.7.cloned.1.call-done = bf16[2048,512]{0,1:T(8,128)(2,1)} async-done(((bf16[128,512]{0,1:T(8,128)(2,1)}), bf16[2048,512]{0,1:T(8,128)(2,1)}) %all-gather.7.cloned.1.call-update) | async-done | bytes 2097168 | tf_op jit(solution)/shard_map/all_gather | solution.py:20
  159.3 2.7 fusion.15
  165.6 2.4 convolution_multiply_fusion.1
  170.4 39.5 %reduce-scatter.5.cloned.1.call-done = bf16[4,16,2048]{2,1,0:T(8,128)(2,1)} async-done(((bf16[32,16,2048]{2,1,0:T(8,128)(2,1)}), bf16[4,16,2048]{2,1,0:T(8,128)(2,1)}) %reduce-scatter.5.cloned.1.call-update) | async-done | bytes 262160 | tf_op jit(solution)/shard_map/reduce_scatter | solution.py:43
  210.0 46.5 %reduce-scatter.9.cloned.1.call-done = bf16[4,16,2048]{2,1,0:T(8,128)(2,1)} async-done(((bf16[32,16,2048]{2,1,0:T(8,128)(2,1)}), bf16[4,16,2048]{2,1,0:T(8,128)(2,1)}) %reduce-scatter.9.cloned.1.call-update) | async-done | bytes 262160 | tf_op jit(solution)/shard_map/reduce_scatter | solution.py:43
  256.6 31.1 %reduce-scatter.7.cloned.1.call-done = bf16[1,16,2048]{2,1,0:T(8,128)(2,1)} async-done(((bf16[4,16,2048]{2,1,0:T(8,128)(2,1)}), bf16[1,16,2048]{2,1,0:T(8,128)(2,1)}) %reduce-scatter.7.cloned.1.call-update) | async-done | bytes 65552 | tf_op jit(solution)/shard_map/reduce_scatter | solution.py:43
  287.7 29.8 %reduce-scatter.11.cloned.1.call-done = bf16[1,16,2048]{2,1,0:T(8,128)(2,1)} async-done(((bf16[4,16,2048]{2,1,0:T(8,128)(2,1)}), bf16[1,16,2048]{2,1,0:T(8,128)(2,1)}) %reduce-scatter.11.cloned.1.call-update) | async-done | bytes 65552 | tf_op jit(solution)/shard_map/reduce_scatter | solution.py:43
  318.4 16.1 %all_gather.20 = bf16[4,16,2048]{2,1,0:T(8,128)(2,1)} all-gather(bf16[1,16,2048]{2,1,0:T(8,128)(2,1)S(1)} %get-tuple-element.3), channel_id=1, replica_groups=mesh['agent'=16,'tp_0'=4,'tp_1'=8] {'tp_0'}, dimensions={0}, use_global_device_ids=true | all-gather | bytes 327680 | tf_op jit(solution)/shard_map/all_gather | solution.py:66
  334.5 15.8 %all_gather.22 = bf16[4,16,2048]{2,1,0:T(8,128)(2,1)} all-gather(bf16[1,16,2048]{2,1,0:T(8,128)(2,1)S(1)} %get-tuple-element.2), channel_id=1, replica_groups=mesh['agent'=16,'tp_0'=4,'tp_1'=8] {'tp_0'}, dimensions={0}, use_global_device_ids=true | all-gather | bytes 327680 | tf_op jit(solution)/shard_map/all_gather | solution.py:66
  350.4 1.9 collective-permute-start.2
  352.3 2.4 collective-permute-start.3
  354.7 21.3 %all-gather.9.cloned.1.call-done = bf16[32,16,2048]{2,1,0:T(8,128)(2,1)} async-done(((bf16[4,16,2048]{2,1,0:T(8,128)(2,1)}), bf16[32,16,2048]{2,1,0:T(8,128)(2,1)}) %all-gather.9.cloned.1.call-update) | async-done | bytes 2097168 | tf_op jit(solution)/shard_map/all_gather | solution.py:66
  376.0 3.2 copy.23
  379.2 41.0 %all-gather.11.cloned.1.call-done = bf16[32,16,2048]{2,1,0:T(8,128)(2,1)} async-done(((bf16[4,16,2048]{2,1,0:T(8,128)(2,1)}), bf16[32,16,2048]{2,1,0:T(8,128)(2,1)}) %all-gather.11.cloned.1.call-update) | async-done | bytes 2097168 | tf_op jit(solution)/shard_map/all_gather | solution.py:66
  420.2 1.7 copy.25
  422.0 6.6 %fusion.13 = f32[2048,256]{1,0:T(8,128)} fusion(bf16[512,4096]{1,0:T(8,128)(2,1)} %all-gather.5.cloned.1.call-done, f32[512,256]{1,0:T(8,128)} %copy-done.7, f32[512,256]{1,0:T(8,128)} %copy-done.5, bf16[512,2048]{1,0:T(8,128)(2,1)} %bitcast.41, bf16[2048,512]{0,1:T(8,128)(2,1)} %all-gather.7.cloned.1.call-done), kind=kOutput, calls=%fused_computation.22 | convolution fusion | flops 1075052544 | bytes 8388608 | tf_op jit(solution)/shard_map/dot_general | solution.py:102
  428.6 8.2 %fusion.20 = bf16[1,2048,256]{2,1,0:T(8,128)(2,1)} fusion(f32[2048,256]{1,0:T(8,128)} %fusion.13, bf16[512,4096]{1,0:T(8,128)(2,1)} %all-gather.5.cloned.1.call-done, bf16[2048,256]{1,0:T(8,128)(2,1)} %collective-permute-done.3, bf16[2048,256]{1,0:T(8,128)(2,1)} %collective-permute-done.2, f32[]{:T(128)} %bitcast.1, f32[]{:T(128)} %bitcast, f32[]{:T(128)S(6)} %sub.31, ...), kind=kOutput, calls=%fused_computation.27 | convolution fusion | flops 1081344000 | bytes 12583940 | tf_op jit(solution)/shard_map/dot_general | solution.py:102
  (45 shorter events, 12.5 us)
Async XLA Ops:
  7.2 112.3 %all-gather.5.cloned.1.call-start = ((), (), s32[]{:S(2)}) async-start(), calls=%async_computation.4 | async-start | bytes 4325376 | tf_op jit(solution)/shard_map/all_gather | solution.py:33
  8.8 150.5 %all-gather.7.cloned.1.call-start = ((), (), s32[]{:S(2)}) async-start(), calls=%async_computation.5 | async-start | bytes 2228224 | tf_op jit(solution)/shard_map/all_gather | solution.py:20
  11.3 198.6 %reduce-scatter.5.cloned.1.call-start = ((), (), s32[]{:S(2)}) async-start(), calls=%async_computation.6 | async-start | bytes 2359296 | tf_op jit(solution)/shard_map/reduce_scatter | solution.py:43
  11.4 27.0 %collective-permute-start = (bf16[2048,256]{1,0:T(8,128)(2,1)}, bf16[2048,256]{1,0:T(8,128)(2,1)S(1)}, u32[]{:S(2)}, u32[]{:S(2)}) collective-permute-start(bf16[2048,256]{1,0:T(8,128)(2,1)} %bitcast.44), channel_id=1, source_target_pairs={{0,480},{32,0},{64,32},{96,64},{128,96},{160,128},{192,160},{224,1... | collective-permute-start | bytes 3145736 | tf_op jit(solution)/shard_map/ppermute | solution.py:13
  15.1 27.6 %collective-permute-start.1 = (bf16[2048,256]{1,0:T(8,128)(2,1)}, bf16[2048,256]{1,0:T(8,128)(2,1)S(1)}, u32[]{:S(2)}, u32[]{:S(2)}) collective-permute-start(bf16[2048,256]{1,0:T(8,128)(2,1)} %bitcast.45), channel_id=1, source_target_pairs={{0,32},{32,64},{64,96},{96,128},{128,160},{160,192},{192,224},{224... | collective-permute-start | bytes 3145736 | tf_op jit(solution)/shard_map/ppermute | solution.py:13
  46.1 75.7 %copy-start.2 = (bf16[2048,256]{1,0:T(8,128)(2,1)}, bf16[2048,256]{1,0:T(8,128)(2,1)S(1)}, u32[]{:S(2)}) copy-start(bf16[2048,256]{1,0:T(8,128)(2,1)S(1)} %fusion.2) | copy-start | bytes 3145732
  121.8 40.3 %copy-start.7 = (f32[512,256]{1,0:T(8,128)}, f32[512,256]{1,0:T(8,128)S(1)}, u32[]{:S(2)}) copy-start(f32[512,256]{1,0:T(8,128)S(1)} %convolution_multiply_fusion.3) | copy-start | bytes 1572868
  159.3 2.8 copy-start.4
  162.1 0.8 copy-start.5
  164.4 1.2 copy-start
  164.4 92.1 %reduce-scatter.9.cloned.1.call-start = ((), (), s32[]{:S(2)}) async-start(), calls=%async_computation.9 | async-start | bytes 2359296 | tf_op jit(solution)/shard_map/reduce_scatter | solution.py:43
  165.6 2.4 copy-start.6
  168.0 0.8 copy-start.8
  170.3 147.1 %copy-start.3 = (bf16[1,16,2048]{2,1,0:T(8,128)(2,1)S(1)}, bf16[1,16,2048]{2,1,0:T(8,128)(2,1)}, u32[]{:S(2)}) copy-start(bf16[1,16,2048]{2,1,0:T(8,128)(2,1)} %param.9) | copy-start | bytes 196612
  170.3 180.1 %copy-start.1 = (bf16[1,2048,256]{2,1,0:T(8,128)(2,1)S(1)}, bf16[1,2048,256]{2,1,0:T(8,128)(2,1)}, u32[]{:S(2)}) copy-start(bf16[1,2048,256]{2,1,0:T(8,128)(2,1)} %param.11) | copy-start | bytes 3145732
  170.4 117.3 %reduce-scatter.7.cloned.1.call-start = ((), (), s32[]{:S(2)}) async-start(), calls=%async_computation.7 | async-start | bytes 327680 | tf_op jit(solution)/shard_map/reduce_scatter | solution.py:43
  209.9 107.5 %reduce-scatter.11.cloned.1.call-start = ((), (), s32[]{:S(2)}) async-start(), calls=%async_computation.10 | async-start | bytes 327680 | tf_op jit(solution)/shard_map/reduce_scatter | solution.py:43
  256.5 119.5 %all-gather.9.cloned.1.call-start = ((), (), s32[]{:S(2)}) async-start(), calls=%async_computation.8 | async-start | bytes 2359296 | tf_op jit(solution)/shard_map/all_gather | solution.py:66
  334.5 85.8 %all-gather.11.cloned.1.call-start = ((), (), s32[]{:S(2)}) async-start(), calls=%async_computation.11 | async-start | bytes 2359296 | tf_op jit(solution)/shard_map/all_gather | solution.py:66
  350.4 78.2 %collective-permute-start.2 = (bf16[2048,256]{1,0:T(8,128)(2,1)S(1)}, bf16[2048,256]{1,0:T(8,128)(2,1)}, u32[]{:S(2)}, u32[]{:S(2)}) collective-permute-start(bf16[2048,256]{1,0:T(8,128)(2,1)S(1)} %bitcast.46), channel_id=1, source_target_pairs={{0,480},{32,0},{64,32},{96,64},{128,96},{160,128},{192,160},{224,1... | collective-permute-start | bytes 3145736 | tf_op jit(solution)/shard_map/ppermute | solution.py:13
  352.3 76.2 %collective-permute-start.3 = (bf16[2048,256]{1,0:T(8,128)(2,1)S(1)}, bf16[2048,256]{1,0:T(8,128)(2,1)}, u32[]{:S(2)}, u32[]{:S(2)}) collective-permute-start(bf16[2048,256]{1,0:T(8,128)(2,1)S(1)} %bitcast.47), channel_id=1, source_target_pairs={{0,32},{32,64},{64,96},{96,128},{128,160},{160,192},{192,224},{224... | collective-permute-start | bytes 3145736 | tf_op jit(solution)/shard_map/ppermute | solution.py:13
Sparse Core Ops, SparseCore 0:
  11.7 107.7 all-gather.4
  121.5 37.7 all-gather.6
  164.5 45.3 reduce-scatter.4
  212.6 43.8 reduce-scatter.8
  259.1 28.4 reduce-scatter.6
  290.3 27.0 reduce-scatter.10
  334.6 41.3 all-gather.8
  378.1 42.0 all-gather.10
where the time goes:
time: 444 us
  waiting for transfers between devices  343 us (77%)
  blocking collectives  31.9 us (7%)
  matrix products  23.7 us (5%)
  between operations  16.1 us (4%)
  local copies, waits for them, and re-layouts  11.5 us (3%)
  starting transfers between devices  10.3 us (2%)
  other arithmetic  7.43 us (2%)
    reduce_scatter x4, waiting for transfers between devices, sum_in_order(): pieces = lax.psum_scatter(pieces, axes[k], scatter_dimension=0, tiled=True)  147 us
    all_gather x1, waiting for transfers between devices, side_by_side(): out = lax.all_gather(both, axis, axis=dim, tiled=True)  73.3 us
    all_gather x2, waiting for transfers between devices, gather_in_order(): pieces = lax.all_gather(pieces, axes[k], axis=0, tiled=True)  62.3 us
    all_gather x1, waiting for transfers between devices, gather_turned(): out = lax.all_gather(both, axis, axis=0, tiled=True)  37.5 us
    all_gather x2, blocking collectives, gather_in_order(): pieces = lax.all_gather(pieces, axes[k], axis=0, tiled=True)  31.9 us
    ppermute x4, waiting for transfers between devices, passed_along(): return lax.ppermute(value, axis, pairs)  22.5 us
    dot_general x2, matrix products, weight_grad(): lax.dot_general(whole, dgate, (((0,), (0,)), ((), ())), preferred_element...  14.8 us
    ppermute x4, starting transfers between devices, passed_along(): return lax.ppermute(value, axis, pairs)  9.95 us
  transfers between devices with their start and end apart: 12, of which 10 were waited for; matrix products, arithmetic and copies ran while one was open for 6% of the time, Pallas kernels for 0%

commit v1 on v0

--- a/solution.py
+++ b/solution.py
@@ -5,6 +5,13 @@
 from jax.sharding import PartitionSpec as P
 
 TP = ("tp_0", "tp_1")
+
+
+def all_by_exchange(array, mesh_axis, dim):
+    count = lax.axis_size(mesh_axis)
+    pieces = jnp.stack([array for _ in range(count)])
+    pieces = lax.all_to_all(pieces, mesh_axis, split_axis=0, concat_axis=0)
+    return jnp.concatenate(pieces, axis=dim)
 
 
 def passed_along(value, axis, steps):
@@ -17,7 +24,7 @@
     turned = [jnp.moveaxis(a, dim, 0) for a, dim in zip(arrays, dims)]
     widths = [t[0].size for t in turned]
     both = jnp.concatenate([t.reshape(-1, w) for t, w in zip(turned, widths)], axis=1)
-    out = lax.all_gather(both, axis, axis=0, tiled=True)
+    out = all_by_exchange(both, axis, 0)
     pieces = jnp.split(out, [sum(widths[:k]) for k in range(1, len(widths))], axis=1)
     return tuple(
         (

time: 444 us -> 408 us (0.919)
  waiting for transfers between devices: 343 us -> 295 us
  starting transfers between devices: 10.3 us -> 19.1 us
    all_gather x1 -> x0, waiting for transfers between devices: 37.5 us -> none  [gather_turned(): out = lax.all_gather(both, axis, axis=0, tiled=True)]
    all_gather x1, waiting for transfers between devices: 73.3 us -> 40.6 us  [side_by_side(): out = lax.all_gather(both, axis, axis=dim, tiled=True)]
    ppermute x4, waiting for transfers between devices: 22.5 us -> 47.1 us  [passed_along(): return lax.ppermute(value, axis, pairs)]
    all_to_all x0 -> x1, starting transfers between devices: none -> 9.54 us  [all_by_exchange(): pieces = lax.all_to_all(pieces, mesh_axis, split_axis=0, concat_axis=0)]
  transfers between devices with their start and end apart: 12 -> 12, of which waited for: 10 -> 9; matrix products, arithmetic and copies ran while one was open for 6% -> 7% of each run, Pallas kernels for 0% -> 0%
where the time goes in v1:
time: 408 us; the launch traced here: 407 us
  waiting for transfers between devices  295 us (72%)
  blocking collectives  31 us (8%)
  matrix products  24.4 us (6%)
  starting transfers between devices  19.1 us (5%)
  between operations  16.3 us (4%)
  local copies, waits for them, and re-layouts  12.9 us (3%)
  other arithmetic  8.23 us (2%)
    reduce_scatter x4, waiting for transfers between devices, sum_in_order(): pieces = lax.psum_scatter(pieces, axes[k], scatter_dimension=0, tiled=True)  144 us
    all_gather x2, waiting for transfers between devices, gather_in_order(): pieces = lax.all_gather(pieces, axes[k], axis=0, tiled=True)  63 us
    ppermute x4, waiting for transfers between devices, passed_along(): return lax.ppermute(value, axis, pairs)  47.1 us
    all_gather x1, waiting for transfers between devices, side_by_side(): out = lax.all_gather(both, axis, axis=dim, tiled=True)  40.6 us
    all_gather x2, blocking collectives, gather_in_order(): pieces = lax.all_gather(pieces, axes[k], axis=0, tiled=True)  31 us
    dot_general x2, matrix products, weight_grad(): lax.dot_general(whole, dgate, (((0,), (0,)), ((), ())), preferred_element...  14.8 us
    all_to_all x1, starting transfers between devices, all_by_exchange(): pieces = lax.all_to_all(pieces, mesh_axis, split_axis=0, concat_axis=0)  9.54 us
    ppermute x4, starting transfers between devices, passed_along(): return lax.ppermute(value, axis, pairs)  9.34 us
  transfers between devices with their start and end apart: 12, of which 9 were waited for; matrix products, arithmetic and copies ran while one was open for 7% of the time, Pallas kernels for 0%

profile of v1, /device:TPU:2, one launch (start us, length us, event | category | flops | bytes accessed | tf_op | source)
XLA Modules:
  0.0 406.9 jit_solution(11137534819100185359)
XLA Ops:
  12.3 9.5 %all-to-all-start = ((bf16[16,128,512]{2,1,0:T(8,128)(2,1)}), bf16[16,128,512]{2,1,0:T(8,128)(2,1)S(1)}, u32[]{:S(2)}, u32[]{:S(2)}) async-start(bf16[16,128,512]{2,1,0:T(8,128)(2,1)} %stack.2), calls=%async_computation | async-start | bytes 4194304 | tf_op jit(solution)/shard_map/all_to_all | solution.py:13
  21.9 3.1 collective-permute-start
  24.9 1.9 collective-permute-start.1
  29.6 43.7 %collective-permute-done = bf16[2048,256]{1,0:T(8,128)(2,1)} collective-permute-done((bf16[2048,256]{1,0:T(8,128)(2,1)S(1)}, bf16[2048,256]{1,0:T(8,128)(2,1)}, u32[]{:S(2)}, u32[]{:S(2)}) %collective-permute-start) | collective-permute-done | bytes 1048608 | tf_op jit(solution)/shard_map/ppermute | solution.py:20
  73.2 3.4 collective-permute-done.1
  76.7 4.9 %fusion.2 = bf16[2048,256]{1,0:T(8,128)(2,1)} fusion(bf16[2048,256]{1,0:T(8,128)(2,1)} %collective-permute-done.1, bf16[2048,256]{1,0:T(8,128)(2,1)} %collective-permute-done, f32[]{:T(128)} %bitcast.36, f32[]{:T(128)} %bitcast.1, f32[]{:T(128)} %bitcast, f32[]{:T(128)S(6)} %sub.31, bf16[1,2048,256]{2,1,0:T(8,128)(2,1)} %param.11, ...), kind=kLoop, calls=%fused_computation.7 | loop fusion | flops 6291456 | bytes 5242896 | tf_op jit(solution)/shard_map/convert_element_type | solution.py:128
  81.6 40.6 %all-gather.4.cloned.1.call-done = bf16[512,4096]{1,0:T(8,128)(2,1)} async-done(((bf16[16,4096]{1,0:T(8,128)(2,1)}), bf16[512,4096]{1,0:T(8,128)(2,1)}) %all-gather.4.cloned.1.call-update) | async-done | bytes 4194320 | tf_op jit(solution)/shard_map/all_gather | solution.py:40
  122.2 3.4 convolution_multiply_fusion.3
  125.6 2.4 fusion.15
  130.4 2.4 convolution_multiply_fusion.1
  135.2 36.3 %reduce-scatter.5.cloned.1.call-done = bf16[4,16,2048]{2,1,0:T(8,128)(2,1)} async-done(((bf16[32,16,2048]{2,1,0:T(8,128)(2,1)}), bf16[4,16,2048]{2,1,0:T(8,128)(2,1)}) %reduce-scatter.5.cloned.1.call-update) | async-done | bytes 262160 | tf_op jit(solution)/shard_map/reduce_scatter | solution.py:50
  171.5 47.1 %reduce-scatter.9.cloned.1.call-done = bf16[4,16,2048]{2,1,0:T(8,128)(2,1)} async-done(((bf16[32,16,2048]{2,1,0:T(8,128)(2,1)}), bf16[4,16,2048]{2,1,0:T(8,128)(2,1)}) %reduce-scatter.9.cloned.1.call-update) | async-done | bytes 262160 | tf_op jit(solution)/shard_map/reduce_scatter | solution.py:50
  218.6 30.9 %reduce-scatter.7.cloned.1.call-done = bf16[1,16,2048]{2,1,0:T(8,128)(2,1)} async-done(((bf16[4,16,2048]{2,1,0:T(8,128)(2,1)}), bf16[1,16,2048]{2,1,0:T(8,128)(2,1)}) %reduce-scatter.7.cloned.1.call-update) | async-done | bytes 65552 | tf_op jit(solution)/shard_map/reduce_scatter | solution.py:50
  249.6 29.9 %reduce-scatter.11.cloned.1.call-done = bf16[1,16,2048]{2,1,0:T(8,128)(2,1)} async-done(((bf16[4,16,2048]{2,1,0:T(8,128)(2,1)}), bf16[1,16,2048]{2,1,0:T(8,128)(2,1)}) %reduce-scatter.11.cloned.1.call-update) | async-done | bytes 65552 | tf_op jit(solution)/shard_map/reduce_scatter | solution.py:50
  280.4 15.8 %all_gather.16 = bf16[4,16,2048]{2,1,0:T(8,128)(2,1)} all-gather(bf16[1,16,2048]{2,1,0:T(8,128)(2,1)S(1)} %get-tuple-element.3), channel_id=1, replica_groups=mesh['agent'=16,'tp_0'=4,'tp_1'=8] {'tp_0'}, dimensions={0}, use_global_device_ids=true | all-gather | bytes 327680 | tf_op jit(solution)/shard_map/all_gather | solution.py:73
  296.2 15.2 %all_gather.18 = bf16[4,16,2048]{2,1,0:T(8,128)(2,1)} all-gather(bf16[1,16,2048]{2,1,0:T(8,128)(2,1)S(1)} %get-tuple-element.2), channel_id=1, replica_groups=mesh['agent'=16,'tp_0'=4,'tp_1'=8] {'tp_0'}, dimensions={0}, use_global_device_ids=true | all-gather | bytes 327680 | tf_op jit(solution)/shard_map/all_gather | solution.py:73
  311.5 1.9 collective-permute-start.2
  313.4 2.4 collective-permute-start.3
  315.8 22.0 %all-gather.6.cloned.1.call-done = bf16[32,16,2048]{2,1,0:T(8,128)(2,1)} async-done(((bf16[4,16,2048]{2,1,0:T(8,128)(2,1)}), bf16[32,16,2048]{2,1,0:T(8,128)(2,1)}) %all-gather.6.cloned.1.call-update) | async-done | bytes 2097168 | tf_op jit(solution)/shard_map/all_gather | solution.py:73
  337.8 3.2 copy.27
  341.1 41.0 %all-gather.8.cloned.1.call-done = bf16[32,16,2048]{2,1,0:T(8,128)(2,1)} async-done(((bf16[4,16,2048]{2,1,0:T(8,128)(2,1)}), bf16[32,16,2048]{2,1,0:T(8,128)(2,1)}) %all-gather.8.cloned.1.call-update) | async-done | bytes 2097168 | tf_op jit(solution)/shard_map/all_gather | solution.py:73
  382.1 3.2 copy.29
  385.3 6.2 %fusion.13 = f32[2048,256]{1,0:T(8,128)} fusion(bf16[512,4096]{1,0:T(8,128)(2,1)} %all-gather.4.cloned.1.call-done, f32[512,256]{1,0:T(8,128)} %convolution_multiply_fusion.3, f32[512,256]{1,0:T(8,128)} %copy-done.4, bf16[512,2048]{1,0:T(8,128)(2,1)} %bitcast.47, bf16[2048,512]{1,0:T(8,128)(2,1)S(1)} %bitcast.42), kind=kOutput, calls=%fused_computation.22 | convolution fusion | flops 1075052544 | bytes 8388608 | tf_op jit(solution)/shard_map/dot_general | solution.py:109
  391.5 8.6 %fusion.20 = bf16[1,2048,256]{2,1,0:T(8,128)(2,1)} fusion(f32[2048,256]{1,0:T(8,128)} %fusion.13, bf16[512,4096]{1,0:T(8,128)(2,1)} %all-gather.4.cloned.1.call-done, bf16[2048,256]{1,0:T(8,128)(2,1)} %collective-permute-done.3, bf16[2048,256]{1,0:T(8,128)(2,1)} %collective-permute-done.2, f32[]{:T(128)} %bitcast.1, f32[]{:T(128)} %bitcast, f32[]{:T(128)S(6)} %sub.31, ...), kind=kOutput, calls=%fused_computation.27 | convolution fusion | flops 1081344000 | bytes 12583940 | tf_op jit(solution)/shard_map/dot_general | solution.py:109
  (44 shorter events, 11.6 us)
Async XLA Ops:
  7.2 115.1 %all-gather.4.cloned.1.call-start = ((), (), s32[]{:S(2)}) async-start(), calls=%async_computation.5 | async-start | bytes 4325376 | tf_op jit(solution)/shard_map/all_gather | solution.py:40
  12.3 9.6 %copy-start = (bf16[1,2048,256]{2,1,0:T(8,128)(2,1)S(1)}, bf16[1,2048,256]{2,1,0:T(8,128)(2,1)}, u32[]{:S(2)}) copy-start(bf16[1,2048,256]{2,1,0:T(8,128)(2,1)} %param.10) | copy-start | bytes 3145732
  12.3 15.3 %copy-start.3 = (f32[16]{0:T(128)S(1)}, f32[16]{0:T(128)}, u32[]{:S(2)}) copy-start(f32[16]{0:T(128)} %param.14) | copy-start | bytes 196
  12.3 113.3 %all-to-all-start = ((bf16[16,128,512]{2,1,0:T(8,128)(2,1)}), bf16[16,128,512]{2,1,0:T(8,128)(2,1)S(1)}, u32[]{:S(2)}, u32[]{:S(2)}) async-start(bf16[16,128,512]{2,1,0:T(8,128)(2,1)} %stack.2), calls=%async_computation | async-start | bytes 4194304 | tf_op jit(solution)/shard_map/all_to_all | solution.py:13
  21.8 149.6 %reduce-scatter.5.cloned.1.call-start = ((), (), s32[]{:S(2)}) async-start(), calls=%async_computation.6 | async-start | bytes 2359296 | tf_op jit(solution)/shard_map/reduce_scatter | solution.py:50
  21.9 51.4 %collective-permute-start = (bf16[2048,256]{1,0:T(8,128)(2,1)S(1)}, bf16[2048,256]{1,0:T(8,128)(2,1)}, u32[]{:S(2)}, u32[]{:S(2)}) collective-permute-start(bf16[2048,256]{1,0:T(8,128)(2,1)S(1)} %bitcast.50), channel_id=1, source_target_pairs={{0,480},{32,0},{64,32},{96,64},{128,96},{160,128},{192,160},{224,1... | collective-permute-start | bytes 3145736 | tf_op jit(solution)/shard_map/ppermute | solution.py:20
  24.9 51.7 %collective-permute-start.1 = (bf16[2048,256]{1,0:T(8,128)(2,1)S(1)}, bf16[2048,256]{1,0:T(8,128)(2,1)}, u32[]{:S(2)}, u32[]{:S(2)}) collective-permute-start(bf16[2048,256]{1,0:T(8,128)(2,1)S(1)} %bitcast.51), channel_id=1, source_target_pairs={{0,32},{32,64},{64,96},{96,128},{128,160},{160,192},{192,224},{224... | collective-permute-start | bytes 3145736 | tf_op jit(solution)/shard_map/ppermute | solution.py:20
  125.6 2.4 copy-start.6
  128.0 0.9 copy-start.4
  130.3 88.2 %reduce-scatter.9.cloned.1.call-start = ((), (), s32[]{:S(2)}) async-start(), calls=%async_computation.9 | async-start | bytes 2359296 | tf_op jit(solution)/shard_map/reduce_scatter | solution.py:50
  130.4 2.4 copy-start.5
  132.8 0.8 copy-start.7
  135.1 144.4 %copy-start.2 = (bf16[1,16,2048]{2,1,0:T(8,128)(2,1)S(1)}, bf16[1,16,2048]{2,1,0:T(8,128)(2,1)}, u32[]{:S(2)}) copy-start(bf16[1,16,2048]{2,1,0:T(8,128)(2,1)} %param.9) | copy-start | bytes 196612
  135.1 176.4 %copy-start.1 = (bf16[1,2048,256]{2,1,0:T(8,128)(2,1)S(1)}, bf16[1,2048,256]{2,1,0:T(8,128)(2,1)}, u32[]{:S(2)}) copy-start(bf16[1,2048,256]{2,1,0:T(8,128)(2,1)} %param.11) | copy-start | bytes 3145732
  135.1 114.5 %reduce-scatter.7.cloned.1.call-start = ((), (), s32[]{:S(2)}) async-start(), calls=%async_computation.7 | async-start | bytes 327680 | tf_op jit(solution)/shard_map/reduce_scatter | solution.py:50
  171.4 108.0 %reduce-scatter.11.cloned.1.call-start = ((), (), s32[]{:S(2)}) async-start(), calls=%async_computation.10 | async-start | bytes 327680 | tf_op jit(solution)/shard_map/reduce_scatter | solution.py:50
  218.6 119.3 %all-gather.6.cloned.1.call-start = ((), (), s32[]{:S(2)}) async-start(), calls=%async_computation.8 | async-start | bytes 2359296 | tf_op jit(solution)/shard_map/all_gather | solution.py:73
  296.2 85.9 %all-gather.8.cloned.1.call-start = ((), (), s32[]{:S(2)}) async-start(), calls=%async_computation.11 | async-start | bytes 2359296 | tf_op jit(solution)/shard_map/all_gather | solution.py:73
  311.5 80.0 %collective-permute-start.2 = (bf16[2048,256]{1,0:T(8,128)(2,1)S(1)}, bf16[2048,256]{1,0:T(8,128)(2,1)}, u32[]{:S(2)}, u32[]{:S(2)}) collective-permute-start(bf16[2048,256]{1,0:T(8,128)(2,1)S(1)} %bitcast.52), channel_id=1, source_target_pairs={{0,480},{32,0},{64,32},{96,64},{128,96},{160,128},{192,160},{224,1... | collective-permute-start | bytes 3145736 | tf_op jit(solution)/shard_map/ppermute | solution.py:20
  313.4 78.1 %collective-permute-start.3 = (bf16[2048,256]{1,0:T(8,128)(2,1)S(1)}, bf16[2048,256]{1,0:T(8,128)(2,1)}, u32[]{:S(2)}, u32[]{:S(2)}) collective-permute-start(bf16[2048,256]{1,0:T(8,128)(2,1)S(1)} %bitcast.53), channel_id=1, source_target_pairs={{0,32},{32,64},{64,96},{96,128},{128,160},{160,192},{192,224},{224... | collective-permute-start | bytes 3145736 | tf_op jit(solution)/shard_map/ppermute | solution.py:20
Sparse Core Ops, SparseCore 0:
  11.7 110.4 all-gather.3
  130.5 40.9 reduce-scatter.4
  174.3 44.2 reduce-scatter.8
  221.2 28.3 reduce-scatter.6
  252.2 27.1 reduce-scatter.10
  296.3 41.5 all-gather.5
  339.9 42.0 all-gather.7
